TPU v7x, 32 devices: a whole 2x2x4 slice. The times are simulated.
32 devices in a mesh: rep: 2 (over y), span: 2 (over core), seq: 4 (over z), tp: 2 (over x).
Axes of the slice: x: 2, y: 2, z: 4, core: 2. Of those that a mesh axis runs over, the one named last changes fastest.
Arguments:
- queries: bfloat16 [8, 512, 24, 128], P(('rep', 'span'), 'seq', 'tp'), parts along dimension 0, may hold values from -110 to 110
- key_states: bfloat16 [8, 512, 4, 128], P(('rep', 'span'), 'seq', 'tp'), parts along dimension 0, may hold values from -11 to 11
- value_states: bfloat16 [8, 512, 4, 128], P(('rep', 'span'), 'seq', 'tp'), parts along dimension 0, may hold values from -6 to 6
- out_weight: bfloat16 [3072, 6144], P('tp', 'seq'), may hold values from -0.109375 to 0.109375
- noise_table: float32 [64, 6144], P(None, 'tp'), may hold values from 0.5 to 2
- plan: int32 [8], P('rep'), parts along dimension 0, may hold values from 0 to 63
Outputs:
- branch_out: bfloat16 [8, 512, 6144], P(('rep', 'span'), 'seq', 'tp'), parts along dimension 0
There are 2 independent parts, one for each index of `rep`. A program takes and returns all parts, laid end to end along the dimension named above; an argument that names none is the same for every part. Nothing has to cross between parts.
All inputs are finite; a program needn't handle non-finite values.
Results may differ from a plain program's by a relative error of at most 0.014.
Values may be sent and summed in bfloat16 or wider, within the bound.
A program may use at most 128 MiB of HBM per device.

v0:
```python
import jax
import jax.numpy as jnp
from jax import lax
from jax.sharding import PartitionSpec as P


def fold_block(carried, query_rows, key_rows, value_rows, factor):
    maxima, totals, weighted = carried
    scores = (
        jnp.einsum("tkgd,skd->tkgs", query_rows, key_rows, preferred_element_type=jnp.float32)
        * factor
    )
    highest = jnp.maximum(maxima, jnp.max(scores, axis=-1))
    shrink = jnp.exp(maxima - highest)
    weights = jnp.exp(scores - highest[..., None])
    totals = totals * shrink + jnp.sum(weights, axis=-1)
    weighted = weighted * shrink[..., None] + jnp.einsum(
        "tkgs,skd->tkgd",
        weights.astype(jnp.bfloat16),
        value_rows,
        preferred_element_type=jnp.float32,
    )
    return (maxima * 0.0 + highest, totals, weighted)


def per_device(queries, key_states, value_states, out_weight, noise_table, plan):
    ch_dev, tok_dev, heads_local, head_size = queries.shape
    kv_local = key_states.shape[2]
    per_kv = heads_local // kv_local
    span_count = ch_dev * lax.axis_size("span")
    first_span = lax.axis_index("span") * ch_dev
    factor = head_size ** (-0.5)
    grouped = queries.reshape(ch_dev, tok_dev, kv_local, per_kv, head_size)
    start_max = jnp.full((ch_dev, tok_dev, kv_local, per_kv), -1e30, jnp.float32)
    start_tot = jnp.zeros((ch_dev, tok_dev, kv_local, per_kv), jnp.float32)
    start_acc = jnp.zeros((ch_dev, tok_dev, kv_local, per_kv, head_size), jnp.float32)
    span_rows = (
        lax.all_gather(key_states, "seq", axis=1, tiled=True),
        lax.all_gather(value_states, "seq", axis=1, tiled=True),
    )
    key_piece = lax.all_gather(span_rows[0], "span", axis=0, tiled=True)
    value_piece = lax.all_gather(span_rows[1], "span", axis=0, tiled=True)
    new_max = []
    new_tot = []
    new_acc = []
    for q_span in range(ch_dev):
        inner_state = (start_max[q_span], start_tot[q_span], start_acc[q_span])
        for k_span in range(span_count):

            def update(inner, q_span=q_span, k_span=k_span):
                return fold_block(
                    inner, grouped[q_span], key_piece[k_span], value_piece[k_span], factor
                )

            inner_state = lax.cond(
                k_span <= first_span + q_span, update, lambda inner: inner, inner_state
            )
        new_max.append(inner_state[0])
        new_tot.append(inner_state[1])
        new_acc.append(inner_state[2])
    attn = (
        (jnp.stack(new_acc) / jnp.stack(new_tot)[..., None])
        .reshape(ch_dev, tok_dev, heads_local * head_size)
        .astype(jnp.bfloat16)
    )
    columns = jnp.einsum(
        "ctf,fo->cto",
        lax.all_gather(attn, "seq", axis=1, tiled=True),
        out_weight,
        preferred_element_type=jnp.float32,
    )
    partial_out = lax.all_to_all(
        columns.astype(jnp.bfloat16), "seq", split_axis=1, concat_axis=2, tiled=True
    ).astype(columns.dtype)
    summed = lax.psum_scatter(
        partial_out.astype(jnp.bfloat16), "tp", scatter_dimension=2, tiled=True
    ).astype(jnp.float32)
    levels = lax.dynamic_slice_in_dim(plan, first_span, ch_dev)
    picks = (levels[:, None] == jnp.arange(noise_table.shape[0], dtype=jnp.int32)[None, :]).astype(
        jnp.float32
    )
    gates = jnp.dot(picks, noise_table, precision=lax.Precision.HIGHEST)
    return (summed * gates[:, None, :]).astype(jnp.bfloat16)


def solution(mesh):
    placed = (
        P(("rep", "span"), "seq", "tp", None),
        P(("rep", "span"), "seq", "tp", None),
        P(("rep", "span"), "seq", "tp", None),
        P("tp", "seq"),
        P(None, "tp"),
        P("rep"),
    )
    return jax.shard_map(
        per_device,
        mesh=mesh,
        in_specs=placed,
        out_specs=P(("rep", "span"), "seq", "tp"),
        check_vma=False,
    )
```

profile of v0, /device:TPU:0, one launch (start us, length us, event | category | flops | bytes accessed | tf_op | source)
XLA Modules:
  0.0 320.5 jit_solution(18199733619609409647)
XLA Ops:
  6.5 0.0 copy-start
  6.5 0.0 all-gather.4.cloned.1.call-start
  6.5 1.0 copy.63
  7.5 18.0 %all_gather.15 = bf16[2,512,2,128]{3,1,2,0:T(8,128)(2,1)} all-gather(bf16[2,128,2,128]{3,1,2,0:T(8,128)(2,1)S(1)} %copy.63), channel_id=1, replica_groups=mesh['rep'=2,'span'=2,'seq'=4,'tp'=2] {'seq'}, dimensions={1}, use_global_device_ids=true | all-gather | bytes 655360 | tf_op jit(solution)/shard_map/all_gather | solution.py:38
  25.5 0.0 all-gather.4.cloned.1.call-update
  25.6 0.0 all-gather.6.cloned.1.call-start
  25.6 0.9 copy.64
  26.5 17.0 %all_gather.17 = bf16[2,512,2,128]{3,1,2,0:T(8,128)(2,1)} all-gather(bf16[2,128,2,128]{3,1,2,0:T(8,128)(2,1)S(1)} %copy.64), channel_id=1, replica_groups=mesh['rep'=2,'span'=2,'seq'=4,'tp'=2] {'seq'}, dimensions={1}, use_global_device_ids=true | all-gather | bytes 655360 | tf_op jit(solution)/shard_map/all_gather | solution.py:39
  43.6 0.0 all-gather.6.cloned.1.call-update
  43.6 0.0 all-gather.8.cloned.1.call-start
  43.7 0.0 all-gather.4.cloned.1.call-done
  43.7 9.6 %all-gather.6.cloned.1.call-done = bf16[4,512,2,128]{3,1,2,0:T(8,128)(2,1)} async-done(((bf16[2,512,2,128]{3,1,2,0:T(8,128)(2,1)}), bf16[4,512,2,128]{3,1,2,0:T(8,128)(2,1)}) %all-gather.6.cloned.1.call-update) | async-done | bytes 1048592 | tf_op jit(solution)/shard_map/all_gather | solution.py:42
  53.3 6.1 %conditional.12 = (f32[128,2,6]{0,2,1:T(8,128)}, f32[128,2,6]{0,2,1:T(8,128)S(1)}, f32[128,2,6,128]{3,0,2,1:T(8,128)S(1)}) conditional(s32[]{:T(128)} %convert_element_type.70, () %tuple.93, (bf16[4,512,2,128]{3,1,2,0:T(8,128)(2,1)}, bf16[2,128,2,6,128]{4,1,3,2,0:T(8,128)(2,1)}, bf16[4,512,2,128]{3,1,2,0:T(8,128)(2,1)}) %tuple.190), branch_computations={%region_16.0_spmd, %region_17.0_spmd} | conditional | flops 409147392 | bytes 11210776 | solution.py:55
  53.3 1.7 bitcast_reduce_fusion.4
  55.0 0.6 exponential_multiply_fusion.1
  55.6 1.2 fusion.85
  56.8 0.7 fusion.104
  57.5 1.9 fusion.93
  59.4 6.2 %conditional.13 = ((f32[128,2,6]{0,2,1:T(8,128)}, f32[128,2,6]{0,2,1:T(8,128)S(1)}, f32[128,2,6,128]{3,0,2,1:T(8,128)S(1)})) conditional(s32[]{:T(128)} %convert_element_type.69, (f32[128,2,6]{0,2,1:T(8,128)}, f32[128,2,6]{0,2,1:T(8,128)S(1)}, f32[128,2,6,128]{3,0,2,1:T(8,128)S(1)}) %conditional.12, (f32[128,2,6]{0,2,1:T(8,128)}, ...), branch_computations={%region_20.0_spmd, %region_21.0_spmd} | conditional | flops 409344000 | bytes 12032032 | solution.py:55
  59.4 1.7 bitcast_reduce_fusion.5
  61.1 0.7 multiply_add_fusion.5
  61.8 0.5 fusion.107
  62.3 0.7 multiply_add_fusion.4
  63.0 0.6 copy.113
  63.6 2.0 fusion.115
  65.6 6.1 %conditional.8 = (f32[128,2,6]{0,2,1:T(8,128)}, f32[128,2,6]{0,2,1:T(8,128)S(1)}, f32[128,2,6,128]{3,0,2,1:T(8,128)S(1)}) conditional(s32[]{:T(128)} %convert_element_type.66, () %tuple.87, (bf16[4,512,2,128]{3,1,2,0:T(8,128)(2,1)}, bf16[2,128,2,6,128]{4,1,3,2,0:T(8,128)(2,1)}, bf16[4,512,2,128]{3,1,2,0:T(8,128)(2,1)}) %tuple.193), branch_computations={%region_0.0_spmd, %region_1.0_spmd} | conditional | flops 409147392 | bytes 11210776 | solution.py:55
  65.6 1.7 bitcast_reduce_fusion
  67.3 0.6 exponential_multiply_fusion
  67.9 1.2 fusion.2
  69.1 0.7 fusion.21
  69.8 1.9 fusion.10
  71.8 0.2 conditional.10
  72.0 1.5 conditional.15
  72.0 0.3 copy.68
  72.2 1.2 copy.102
  73.4 1.4 conditional.11
  73.4 0.3 copy.65
  73.7 1.2 copy.100
  74.9 0.1 div.11
  75.0 1.6 copy.73
  76.6 2.9 fusion.171
  79.5 0.0 all-gather.8.cloned.1.call-update
  79.6 0.0 reduce-scatter.2.cloned.1.call-start
  79.6 93.0 %all-gather.8.cloned.1.call-done = bf16[2,512,1536]{2,1,0:T(8,128)(2,1)} async-done(((bf16[2,128,1536]{2,1,0:T(8,128)(2,1)}), bf16[2,512,1536]{2,1,0:T(8,128)(2,1)}) %all-gather.8.cloned.1.call-update) | async-done | bytes 3145744 | tf_op jit(solution)/shard_map/all_gather | solution.py:68
  172.6 8.1 %fusion.168 = bf16[2,512,1536]{2,1,0:T(8,128)(2,1)S(1)} fusion(bf16[2,512,1536]{2,1,0:T(8,128)(2,1)} %all-gather.8.cloned.1.call-done, bf16[1536,1536]{1,0:T(8,128)(2,1)} %param.25), kind=kOutput, calls=%fused_computation.166 | convolution fusion | flops 4833411072 | bytes 11010048 | tf_op jit(solution)/shard_map/ctf,fo->cto/dot_general | solution.py:66
  180.7 3.2 %copy.74 = bf16[2,512,1536]{2,0,1:T(2,128)(2,1)S(1)} copy(bf16[2,512,1536]{2,1,0:T(8,128)(2,1)S(1)} %fusion.168) | data formatting | bytes 6291456 | tf_op jit(solution)/shard_map/convert_element_type | solution.py:73
  183.9 73.3 %all_to_all.18 = bf16[2,512,1536]{2,0,1:T(2,128)(2,1)S(1)} all-to-all(bf16[2,512,1536]{2,0,1:T(2,128)(2,1)S(1)} %copy.74), channel_id=1, replica_groups=mesh['rep'=2,'span'=2,'seq'=4,'tp'=2] {'seq'}, dimensions={1} | all-to-all | bytes 6291456 | tf_op jit(solution)/shard_map/all_to_all | solution.py:72
  257.2 4.1 %copy.75 = bf16[2,128,4,1536]{3,2,1,0:T(4,128)(2,1)} copy(bf16[2,128,4,1536]{3,0,1,2:T(2,128)(2,1)S(1)} %bitcast.326) | data formatting | bytes 6291456 | tf_op jit(solution)/shard_map/all_to_all | solution.py:72
  261.3 6.9 %all_to_all.16 = bf16[2,128,6144]{2,1,0:T(8,128)(2,1)} reshape(bf16[2,128,4,1536]{3,2,1,0:T(4,128)(2,1)} %copy.75) | data formatting | bytes 6291456 | tf_op jit(solution)/shard_map/all_to_all | solution.py:72
  268.3 0.0 copy-start.5
  268.3 0.0 reduce-scatter.2.cloned.1.call-update
  268.3 0.6 copy-done.5
  268.9 0.1 dynamic_slice.3
  269.0 0.0 copy-done
  269.0 0.4 fusion.172
  269.4 41.7 %reduce-scatter.2.cloned.1.call-done = bf16[2,128,3072]{2,1,0:T(8,128)(2,1)} async-done(((bf16[2,128,6144]{2,1,0:T(8,128)(2,1)}), bf16[2,128,3072]{2,1,0:T(8,128)(2,1)}) %reduce-scatter.2.cloned.1.call-update) | async-done | bytes 1572880 | tf_op jit(solution)/shard_map/reduce_scatter | solution.py:75
  311.1 2.9 multiply_convert_fusion
  (3 shorter events, 0.0 us)
Async XLA Ops:
  6.5 262.4 %copy-start = (f32[64,3072]{1,0:T(8,128)S(1)}, f32[64,3072]{1,0:T(8,128)}, u32[]{:S(2)}) copy-start(f32[64,3072]{1,0:T(8,128)} %param.26) | copy-start | bytes 2359300
  6.5 37.2 %all-gather.4.cloned.1.call-start = ((), (), s32[]{:S(2)}) async-start(), calls=%async_computation.2 | async-start | bytes 1572864 | tf_op jit(solution)/shard_map/all_gather | solution.py:41
  25.6 27.7 %all-gather.6.cloned.1.call-start = ((), (), s32[]{:S(2)}) async-start(), calls=%async_computation.3 | async-start | bytes 1572864 | tf_op jit(solution)/shard_map/all_gather | solution.py:42
  43.6 129.0 %all-gather.8.cloned.1.call-start = ((), (), s32[]{:S(2)}) async-start(), calls=%async_computation.4 | async-start | bytes 3932160 | tf_op jit(solution)/shard_map/all_gather | solution.py:68
  79.6 231.5 %reduce-scatter.2.cloned.1.call-start = ((), (), s32[]{:S(2)}) async-start(), calls=%async_computation.5 | async-start | bytes 4718592 | tf_op jit(solution)/shard_map/reduce_scatter | solution.py:75
  268.3 0.7 copy-start.5
Sparse Core Ops, SparseCore 0:
  25.7 10.8 all-gather.3
  43.7 9.5 all-gather.5
  79.7 92.8 all-gather.7
  268.4 42.6 reduce-scatter.1
where the time goes:
time: 322 us; the launch traced here: 321 us
  waiting for transfers between devices  144 us (45%)
  blocking collectives  108 us (34%)
  local copies, waits for them, and re-layouts  22.1 us (7%)
  matrix products  19.2 us (6%)
  between operations  13.2 us (4%)
  other arithmetic  12.9 us (4%)
    all_gather x1, waiting for transfers between devices, per_device(): lax.all_gather(attn, 'seq', axis=1, tiled=True)  93 us
    all_to_all x1, blocking collectives, per_device(): lax.all_to_all(columns.astype(jnp.bfloat16), 'seq', split_axis=1, concat_...  73.3 us
    reduce_scatter x1, waiting for transfers between devices, per_device(): lax.psum_scatter(partial_out.astype(jnp.bfloat16), 'tp', scatter_dimensio...  41.7 us
    all_gather x1, blocking collectives, per_device(): lax.all_gather(key_states, 'seq', axis=1, tiled=True)  18 us
    all_gather x1, blocking collectives, per_device(): lax.all_gather(value_states, 'seq', axis=1, tiled=True)  17 us
    all_to_all x2, local copies, waits for them, and re-layouts, per_device(): lax.all_to_all(columns.astype(jnp.bfloat16), 'seq', split_axis=1, concat_...  11 us
    all_gather x1, waiting for transfers between devices, per_device(): value_piece = lax.all_gather(span_rows[1], 'span', axis=0, tiled=True)  9.6 us
    dot_general x1, matrix products, per_device(): jnp.einsum('ctf,fo->cto', lax.all_gather(attn, 'seq', axis=1, tiled=True)...  8.06 us
  transfers between devices with their start and end apart: 4, of which 3 were waited for; matrix products, arithmetic and copies ran while one was open for 0% of the time, Pallas kernels for 0%

commit v1 on v0

--- a/solution.py
+++ b/solution.py
@@ -69,9 +69,14 @@
         out_weight,
         preferred_element_type=jnp.float32,
     )
-    partial_out = lax.all_to_all(
-        columns.astype(jnp.bfloat16), "seq", split_axis=1, concat_axis=2, tiled=True
-    ).astype(columns.dtype)
+
+    def _cover_forms(page, row_dim, pos_dim):
+        return jnp.concatenate(
+            lax.all_to_all(jnp.stack(jnp.split(page, lax.axis_size("seq"), row_dim)), "seq", 0, 0),
+            pos_dim,
+        )
+
+    partial_out = _cover_forms(columns.astype(jnp.bfloat16), 1, 2).astype(columns.dtype)
     summed = lax.psum_scatter(
         partial_out.astype(jnp.bfloat16), "tp", scatter_dimension=2, tiled=True
     ).astype(jnp.float32)

time: 322 us -> 314 us (0.975)
  local copies, waits for them, and re-layouts: 22.1 us -> 14.3 us
    all_to_all x2 -> x0, local copies, waits for them, and re-layouts: 11 us -> none  [per_device(): lax.all_to_all(columns.astype(jnp.bfloat16), 'seq', split_axis=1, concat_...]
    reshape x0 -> x1, local copies, waits for them, and re-layouts: none -> 4.65 us  [_cover_forms(): jnp.concatenate(lax.all_to_all(jnp.stack(jnp.split(page, lax.axis_size('s...]
where the time goes in v1:
time: 314 us; the launch traced here: 313 us
  waiting for transfers between devices  144 us (46%)
  blocking collectives  109 us (35%)
  matrix products  19.2 us (6%)
  local copies, waits for them, and re-layouts  14.3 us (5%)
  between operations  13.2 us (4%)
  other arithmetic  12.5 us (4%)
    all_gather x1, waiting for transfers between devices, per_device(): lax.all_gather(attn, 'seq', axis=1, tiled=True)  93 us
    all_to_all x1, blocking collectives, _cover_forms(): lax.all_to_all(jnp.stack(jnp.split(page, lax.axis_size('seq'), row_dim)),...  74.1 us
    reduce_scatter x1, waiting for transfers between devices, per_device(): lax.psum_scatter(partial_out.astype(jnp.bfloat16), 'tp', scatter_dimensio...  41.8 us
    all_gather x1, blocking collectives, per_device(): lax.all_gather(key_states, 'seq', axis=1, tiled=True)  18 us
    all_gather x1, blocking collectives, per_device(): lax.all_gather(value_states, 'seq', axis=1, tiled=True)  17 us
    all_gather x1, waiting for transfers between devices, per_device(): value_piece = lax.all_gather(span_rows[1], 'span', axis=0, tiled=True)  9.6 us
    dot_general x1, matrix products, per_device(): jnp.einsum('ctf,fo->cto', lax.all_gather(attn, 'seq', axis=1, tiled=True)...  8.05 us
  transfers between devices with their start and end apart: 4, of which 3 were waited for; matrix products, arithmetic and copies ran while one was open for 0% of the time, Pallas kernels for 0%

profile of v1, /device:TPU:0, one launch (start us, length us, event | category | flops | bytes accessed | tf_op | source)
XLA Modules:
  0.0 313.2 jit_solution(3246276837477421130)
XLA Ops:
  6.5 0.0 copy-start
  6.5 0.0 all-gather.4.cloned.1.call-start
  6.5 1.0 copy.63
  7.5 18.0 %all_gather.15 = bf16[2,512,2,128]{3,1,2,0:T(8,128)(2,1)} all-gather(bf16[2,128,2,128]{3,1,2,0:T(8,128)(2,1)S(1)} %copy.63), channel_id=1, replica_groups=mesh['rep'=2,'span'=2,'seq'=4,'tp'=2] {'seq'}, dimensions={1}, use_global_device_ids=true | all-gather | bytes 655360 | tf_op jit(solution)/shard_map/all_gather | solution.py:38
  25.5 0.0 all-gather.4.cloned.1.call-update
  25.6 0.0 all-gather.6.cloned.1.call-start
  25.6 0.9 copy.64
  26.5 17.0 %all_gather.17 = bf16[2,512,2,128]{3,1,2,0:T(8,128)(2,1)} all-gather(bf16[2,128,2,128]{3,1,2,0:T(8,128)(2,1)S(1)} %copy.64), channel_id=1, replica_groups=mesh['rep'=2,'span'=2,'seq'=4,'tp'=2] {'seq'}, dimensions={1}, use_global_device_ids=true | all-gather | bytes 655360 | tf_op jit(solution)/shard_map/all_gather | solution.py:39
  43.6 0.0 all-gather.6.cloned.1.call-update
  43.6 0.0 all-gather.8.cloned.1.call-start
  43.7 0.0 all-gather.4.cloned.1.call-done
  43.7 9.6 %all-gather.6.cloned.1.call-done = bf16[4,512,2,128]{3,1,2,0:T(8,128)(2,1)} async-done(((bf16[2,512,2,128]{3,1,2,0:T(8,128)(2,1)}), bf16[4,512,2,128]{3,1,2,0:T(8,128)(2,1)}) %all-gather.6.cloned.1.call-update) | async-done | bytes 1048592 | tf_op jit(solution)/shard_map/all_gather | solution.py:42
  53.3 6.1 %conditional.12 = (f32[128,2,6]{0,2,1:T(8,128)}, f32[128,2,6]{0,2,1:T(8,128)S(1)}, f32[128,2,6,128]{3,0,2,1:T(8,128)S(1)}) conditional(s32[]{:T(128)} %convert_element_type.70, () %tuple.93, (bf16[4,512,2,128]{3,1,2,0:T(8,128)(2,1)}, bf16[2,128,2,6,128]{4,1,3,2,0:T(8,128)(2,1)}, bf16[4,512,2,128]{3,1,2,0:T(8,128)(2,1)}) %tuple.193), branch_computations={%region_16.0_spmd, %region_17.0_spmd} | conditional | flops 409147392 | bytes 11210776 | solution.py:55
  53.3 1.7 bitcast_reduce_fusion.4
  55.0 0.6 exponential_multiply_fusion.1
  55.6 1.2 fusion.85
  56.8 0.7 fusion.104
  57.5 1.9 fusion.93
  59.4 6.2 %conditional.13 = ((f32[128,2,6]{0,2,1:T(8,128)}, f32[128,2,6]{0,2,1:T(8,128)S(1)}, f32[128,2,6,128]{3,0,2,1:T(8,128)S(1)})) conditional(s32[]{:T(128)} %convert_element_type.69, (f32[128,2,6]{0,2,1:T(8,128)}, f32[128,2,6]{0,2,1:T(8,128)S(1)}, f32[128,2,6,128]{3,0,2,1:T(8,128)S(1)}) %conditional.12, (f32[128,2,6]{0,2,1:T(8,128)}, ...), branch_computations={%region_20.0_spmd, %region_21.0_spmd} | conditional | flops 409344000 | bytes 12032032 | solution.py:55
  59.4 1.7 bitcast_reduce_fusion.5
  61.1 0.7 multiply_add_fusion.5
  61.8 0.5 fusion.107
  62.3 0.7 multiply_add_fusion.4
  63.0 0.6 copy.113
  63.6 2.0 fusion.115
  65.6 6.1 %conditional.8 = (f32[128,2,6]{0,2,1:T(8,128)}, f32[128,2,6]{0,2,1:T(8,128)S(1)}, f32[128,2,6,128]{3,0,2,1:T(8,128)S(1)}) conditional(s32[]{:T(128)} %convert_element_type.66, () %tuple.87, (bf16[4,512,2,128]{3,1,2,0:T(8,128)(2,1)}, bf16[2,128,2,6,128]{4,1,3,2,0:T(8,128)(2,1)}, bf16[4,512,2,128]{3,1,2,0:T(8,128)(2,1)}) %tuple.196), branch_computations={%region_0.0_spmd, %region_1.0_spmd} | conditional | flops 409147392 | bytes 11210776 | solution.py:55
  65.6 1.7 bitcast_reduce_fusion
  67.3 0.6 exponential_multiply_fusion
  67.9 1.2 fusion.2
  69.1 0.7 fusion.21
  69.8 1.9 fusion.10
  71.8 0.2 conditional.10
  72.0 1.5 conditional.15
  72.0 0.3 copy.68
  72.2 1.2 copy.102
  73.4 1.4 conditional.11
  73.4 0.3 copy.65
  73.7 1.2 copy.100
  74.9 0.1 div.11
  75.0 1.6 copy.73
  76.6 3.0 fusion.171
  79.5 0.0 all-gather.8.cloned.1.call-update
  79.6 0.0 reduce-scatter.2.cloned.1.call-start
  79.6 93.0 %all-gather.8.cloned.1.call-done = bf16[2,512,1536]{2,1,0:T(8,128)(2,1)} async-done(((bf16[2,128,1536]{2,1,0:T(8,128)(2,1)}), bf16[2,512,1536]{2,1,0:T(8,128)(2,1)}) %all-gather.8.cloned.1.call-update) | async-done | bytes 3145744 | tf_op jit(solution)/shard_map/all_gather | solution.py:68
  172.6 8.1 %fusion.168 = bf16[2,512,1536]{2,1,0:T(8,128)(2,1)S(1)} fusion(bf16[2,512,1536]{2,1,0:T(8,128)(2,1)} %all-gather.8.cloned.1.call-done, bf16[1536,1536]{1,0:T(8,128)(2,1)} %param.25), kind=kOutput, calls=%fused_computation.166 | convolution fusion | flops 4833411072 | bytes 11010048 | tf_op jit(solution)/shard_map/ctf,fo->cto/dot_general | solution.py:66
  180.7 0.2 slice_bitcast_fusion.7
  180.9 0.4 pad_maximum_fusion
  181.3 74.1 %all_to_all.5 = bf16[4,2,128,1536]{3,2,1,0:T(8,128)(2,1)} all-to-all(bf16[4,2,128,1536]{3,2,1,0:T(8,128)(2,1)S(1)} %pad_maximum_fusion), channel_id=1, replica_groups=mesh['rep'=2,'span'=2,'seq'=4,'tp'=2] {'seq'}, dimensions={0} | all-to-all | bytes 6291456 | tf_op jit(solution)/shard_map/all_to_all | solution.py:75
  255.4 4.7 %copy.74 = bf16[2,128,4,1536]{1,3,2,0:T(8,128)(2,1)} copy(bf16[2,128,4,1536]{3,1,0,2:T(8,128)(2,1)} %bitcast.334) | data formatting | bytes 6291456 | tf_op jit(solution)/shard_map/reshape | solution.py:74
  260.1 0.0 copy-start.5
  260.1 0.0 reduce-scatter.2.cloned.1.call-update
  260.1 0.6 copy-done.5
  260.8 0.1 dynamic_slice.3
  260.8 0.0 copy-done
  260.8 0.4 fusion.172
  261.2 41.8 %reduce-scatter.2.cloned.1.call-done = bf16[2,128,3072]{1,2,0:T(8,128)(2,1)} async-done(((bf16[2,128,6144]{1,2,0:T(8,128)(2,1)}), bf16[2,128,3072]{1,2,0:T(8,128)(2,1)}) %reduce-scatter.2.cloned.1.call-update) | async-done | bytes 1572880 | tf_op jit(solution)/shard_map/reduce_scatter | solution.py:80
  303.0 2.1 multiply_convert_fusion
  305.1 1.6 copy.75
  (3 shorter events, 0.0 us)
Async XLA Ops:
  6.5 254.3 %copy-start = (f32[64,3072]{1,0:T(8,128)S(1)}, f32[64,3072]{1,0:T(8,128)}, u32[]{:S(2)}) copy-start(f32[64,3072]{1,0:T(8,128)} %param.26) | copy-start | bytes 2359300
  6.5 37.2 %all-gather.4.cloned.1.call-start = ((), (), s32[]{:S(2)}) async-start(), calls=%async_computation.2 | async-start | bytes 1572864 | tf_op jit(solution)/shard_map/all_gather | solution.py:41
  25.6 27.7 %all-gather.6.cloned.1.call-start = ((), (), s32[]{:S(2)}) async-start(), calls=%async_computation.3 | async-start | bytes 1572864 | tf_op jit(solution)/shard_map/all_gather | solution.py:42
  43.6 129.0 %all-gather.8.cloned.1.call-start = ((), (), s32[]{:S(2)}) async-start(), calls=%async_computation.4 | async-start | bytes 3932160 | tf_op jit(solution)/shard_map/all_gather | solution.py:68
  79.6 223.4 %reduce-scatter.2.cloned.1.call-start = ((), (), s32[]{:S(2)}) async-start(), calls=%async_computation.5 | async-start | bytes 4718592 | tf_op jit(solution)/shard_map/reduce_scatter | solution.py:80
  260.1 0.7 copy-start.5
Sparse Core Ops, SparseCore 0:
  25.7 10.8 all-gather.3
  43.7 9.5 all-gather.5
  79.7 92.8 all-gather.7
  260.3 42.6 reduce-scatter.1
